TPU v7x, 512 devices: a whole 4x8x8 slice. The times are simulated.
512 devices in a mesh: row: 16 (over y, core), col: 32 (over z, x).
Axes of the slice: x: 4, y: 8, z: 8, core: 2. Of those that a mesh axis runs over, the one named last changes fastest.
Arguments:
- offsets: float32 [3, 131072], P(None, ('row', 'col')), may hold values from 0 to 11
- cells: int32 [3, 1024], replicated, may hold values from 0 to 15, as said below
- types: int32 [131072], P(('row', 'col')), may hold values from 0 to 3, as said below
- mask: int32 [16, 64, 16, 64], P(None, 'col', 'row'), may hold values from 0 to 1, as said below
- chi_table: float32 [4], replicated, may hold values from 2 to 10.1
- eta_table: float32 [4], replicated, may hold values from 13 to 18
- gamma_table: float32 [4], replicated, may hold values from 0.4 to 0.8
Outputs:
- charges: float32 [131072], P(('row', 'col'))
Inputs may be any that keep to these rules, and one draw needn't show every extreme that they name: The cells of the blocks are a permutation of all 16 x 16 x 4 cells: each cell holds exactly one block. The mask marks a pair of blocks exactly when their cells are equal or adjacent on the periodic grid in every dimension; it is symmetric and each block is marked with exactly 27 blocks, itself included. `types`: types 2 and 3 grow more common along the atoms, from none in the first 256 atoms to nearly all in the last.
All inputs are finite; a program needn't handle non-finite values.
Results may differ from a plain program's by a relative error of at most 0.0003.
Values sent between devices are 32-bit elements; how exact they have to be, the bound alone decides.
A program may use at most 64 MiB of HBM per device.

v0:
```python
import jax
import jax.numpy as jnp
from jax import lax
from jax.sharding import Mesh
from jax.sharding import PartitionSpec as P

BLOCK = 128
GRID_Z = 4
ITERS = 3
ROW_COL = ("row_0", "row_1", "col_0", "col_1")
ROW = ("row_0", "row_1")
COL = ("col_0", "col_1")


coulomb = 14.4
cutoff = 10.0
cell_side = 11.0
pair_group = 64


def copy_for_each(value, axis):
    devices = lax.axis_size(axis)
    return lax.all_to_all(
        jnp.broadcast_to(value[None], (devices, *value.shape)), axis, 0, 0, tiled=True
    )


def over_copies(value, axis):
    return copy_for_each(value, axis).sum(axis=0)


def over_axes(value, axes):
    far, near = axes
    return over_copies(over_copies(value, near), far)


def in_one(arrays, axis):
    line, at, outs = (jnp.concatenate([a.reshape(-1) for a in arrays]), 0, [])
    subtotal = over_axes(line, axis)
    for a in arrays:
        outs.append(subtotal[at : at + a.size].reshape(a.shape))
        at += a.size
    return tuple(outs)


def in_order(blocks, dim):
    blocks = jnp.moveaxis(blocks, 0, dim)
    lengths = blocks.shape
    return blocks.reshape(*lengths[:dim], lengths[dim] * lengths[dim + 1], *lengths[dim + 2 :])


def gathered_copies(value, axis, dim):
    return in_order(copy_for_each(value, axis), dim)


def in_blocks(value, dim, devices):
    before, after = (value.shape[:dim], value.shape[dim + 1 :])
    return jnp.moveaxis(value.reshape(*before, devices, -1, *after), dim, 0)


def sent_and_summed(value, axis, dim):
    devices = lax.axis_size(axis)
    blocks = lax.all_to_all(in_blocks(value, dim, devices), axis, 0, 0, tiled=True)
    return jnp.sum(blocks, axis=0)


def taper(dist):
    xval = dist / cutoff
    poly = 1.0 + xval**4 * (-35.0 + xval * (84.0 + xval * (-70.0 + 20.0 * xval)))
    return jnp.where(xval < 1.0, poly, 0.0)


def coupling(tgt, src, tgt_cell, src_cell, same, grid):
    half = grid[:, None] // 2
    shift = ((src_cell - tgt_cell + half) % grid[:, None] - half).astype(jnp.float32) * cell_side
    radius_sq = jnp.zeros((tgt.shape[1], tgt.shape[2], src.shape[2]), jnp.float32)
    for comp in range(3):
        delta = shift[comp][:, None, None] + src[comp][:, None, :] - tgt[comp][:, :, None]
        radius_sq = radius_sq + delta * delta
    dist = jnp.sqrt(radius_sq)
    paired = tgt[3][:, :, None] * src[3][:, None, :]
    shield = 1.0 / (paired * jnp.sqrt(paired))
    kern = coulomb * taper(dist) / jnp.cbrt(radius_sq * dist + shield)
    width = tgt.shape[2]
    diag = jnp.arange(width)[:, None] == jnp.arange(width)[None, :]
    return jnp.where(same[:, None, None] & diag[None], 0.0, kern)


def pick(kinds, table):
    return jnp.sum(jnp.where(kinds, table[:, None], 0.0), axis=0)


def paired_sums(residual, image):
    return in_one(
        (jnp.sum(residual * residual, axis=1), jnp.sum(residual * image, axis=1)),
        ("row_0", ("row_1", "col_0", "col_1")),
    )


def per_device(offsets, cells, types, mask, chi_table, eta_table, gamma_table):
    n_row = lax.axis_size(ROW)
    n_col = lax.axis_size(COL)
    row_at = lax.axis_index(ROW)
    col_at = lax.axis_index(COL)
    span = types.shape[0]
    bpd = span // BLOCK
    n_tgt = n_row * bpd
    n_src = n_col * bpd
    grid = jnp.array([n_row, n_src // GRID_Z, GRID_Z], jnp.int32)
    kinds = jnp.arange(chi_table.shape[0])[:, None] == types[None, :]
    chi = pick(kinds, chi_table)
    eta = pick(kinds, eta_table)
    gamma = pick(kinds, gamma_table)
    geo = jnp.concatenate([offsets, gamma[None]], axis=0)
    src_geo = gathered_copies(geo, COL, 1).reshape(4, n_src, BLOCK)
    tgt_geo = lax.all_gather(geo, ROW, axis=1, tiled=True).reshape(4, n_tgt, BLOCK)
    tgt_ids = (
        (jnp.arange(n_row, dtype=jnp.int32)[:, None] * n_col + col_at) * bpd
        + jnp.arange(bpd, dtype=jnp.int32)[None, :]
    ).reshape(n_tgt)
    src_ids = row_at * n_src + jnp.arange(n_src, dtype=jnp.int32)
    tgt_cells = jnp.take(cells, tgt_ids, axis=1)
    src_cells = jnp.take(cells, src_ids, axis=1)
    tile = mask.reshape(n_tgt * n_src)
    count = jnp.sum(tile)
    slots = jnp.nonzero(tile, size=n_tgt * n_src + pair_group, fill_value=0)[0].astype(jnp.int32)
    groups = (count + pair_group - 1) // pair_group
    src_range = jnp.arange(n_src, dtype=jnp.int32)

    def block_kernel(step):
        picked = lax.dynamic_slice_in_dim(slots, step * pair_group, pair_group)
        live = step * pair_group + jnp.arange(pair_group) < count
        tgt_blk = picked // n_src
        src_blk = picked % n_src
        kern = coupling(
            tgt_geo[:, tgt_blk],
            src_geo[:, src_blk],
            tgt_cells[:, tgt_blk],
            src_cells[:, src_blk],
            tgt_ids[tgt_blk] == src_ids[src_blk],
            grid,
        )
        return (jnp.where(live[:, None, None], kern, 0.0), tgt_blk, src_blk)

    def apply(direction):
        remote = lax.all_gather(direction, ROW, axis=1, tiled=True).reshape(2, n_tgt, BLOCK)

        def turn(step, acc):
            kern, tgt_blk, src_blk = block_kernel(step)
            contrib = jnp.einsum(
                "gij,kgi->kgj", kern, remote[:, tgt_blk], precision=lax.Precision.HIGHEST
            )
            owners = (src_range[:, None] == src_blk[None, :]).astype(jnp.float32)
            return acc + jnp.einsum("sg,kgj->ksj", owners, contrib, precision=lax.Precision.HIGHEST)

        acc = lax.fori_loop(0, groups, turn, jnp.zeros((2, n_src, BLOCK), jnp.float32))
        summed = sent_and_summed(acc.reshape(2, n_src * BLOCK), COL, 1)
        return summed + eta[None] * direction

    rhs = jnp.stack([-chi, -jnp.ones_like(chi)], axis=0)
    solution = jnp.zeros_like(rhs)
    residual = rhs
    image = apply(residual)
    norm_now, product = paired_sums(residual, image)
    alpha = norm_now / product
    direction = residual
    along = image
    for step in range(ITERS):
        solution = solution + alpha[:, None] * direction
        residual = residual - alpha[:, None] * along
        if step + 1 < ITERS:
            image = apply(residual)
            norm_next, product = paired_sums(residual, image)
            ratio = norm_next / norm_now
            alpha = norm_next / (product - ratio * norm_next / alpha)
            direction = residual + ratio[:, None] * direction
            along = image + ratio[:, None] * along
            norm_now = norm_next
    totals = over_axes(jnp.sum(solution, axis=1), ("row_0", ("row_1", "col_0", "col_1")))
    return solution[0] - totals[0] / totals[1] * solution[1]


def solution(mesh):
    torus = Mesh(mesh.devices.reshape(8, 2, 8, 4), ("row_0", "row_1", "col_0", "col_1"))
    placed = (P(None, ROW_COL), P(), P(ROW_COL), P(None, COL, ROW, None), P(), P(), P())
    return jax.shard_map(
        per_device, mesh=torus, in_specs=placed, out_specs=P(ROW_COL), check_vma=False
    )
```

profile of v0, /device:TPU:1, one launch (start us, length us, event | category | flops | bytes accessed | tf_op | source)
XLA Modules:
  0.0 371.3 jit_solution(4462579200094896409)
XLA Ops:
  0.0 0.8 select_reduce_fusion
  0.8 0.7 pad_maximum_fusion
  1.5 0.7 broadcast_in_dim.293
  2.2 13.7 %all-to-all-start = ((f32[32,4,256]{2,1,0:T(4,128)}), f32[32,4,256]{2,1,0:T(4,128)S(1)}, u32[]{:S(2)}, u32[]{:S(2)}) async-start(f32[32,4,256]{2,1,0:T(4,128)} %broadcast_in_dim.293), calls=%async_computation | async-start | bytes 262144 | tf_op jit(solution)/shard_map/all_to_all | solution.py:23
  15.9 1.4 fusion.201
  18.5 0.6 gather_fusion.21
  19.1 0.6 gather_fusion.22
  19.8 0.3 reduce-window.16
  20.4 14.7 %scatter_custom_fusion = s32[2112]{0:T(1024)S(1)} fusion(s32[2048]{0:T(1024)S(1)} %bitcast.241, s32[2048]{0:T(1024)S(1)} %broadcast.958, s32[]{:T(128)} %constant.520.clone.1), kind=kCustom, calls=%fused_computation.302 | custom fusion | flops 2048 | bytes 8452 | tf_op jit(solution)/shard_map/scatter-add | solution.py:126
  35.7 18.5 %all_gather.12 = f32[2,4096]{1,0:T(2,128)S(1)} all-gather(f32[2,256]{1,0:T(2,128)S(1)} %stack.2), channel_id=1, replica_groups=mesh['row_0'=8,'row_1'=2,'col_0'=8,'col_1'=4] {'row_0','row_1'}, dimensions={1}, use_global_device_ids=true | all-gather | bytes 34816 | tf_op jit(solution)/shard_map/all_gather | solution.py:146
  54.2 0.7 fusion.199
  54.9 15.1 %all_gather.13 = f32[4,4096]{1,0:T(4,128)S(1)} all-gather(f32[4,256]{1,0:T(4,128)S(1)} %pad_maximum_fusion), channel_id=1, replica_groups=mesh['row_0'=8,'row_1'=2,'col_0'=8,'col_1'=4] {'row_0','row_1'}, dimensions={1}, use_global_device_ids=true | all-gather | bytes 69632 | tf_op jit(solution)/shard_map/all_gather | solution.py:116
  70.1 21.0 %while.48 = (s32[]{:T(128)}, f32[2,64,128]{2,1,0:T(8,128)S(1)}, s32[]{:T(128)}, s32[2112]{0:T(1024)S(1)}, f32[2,32,128]{2,0,1:T(2,128)S(1)}, /*index=5*/s32[]{:T...) while((s32[]{:T(128)}, f32[2,64,128]{2,1,0:T(8,128)S(1)}, ...), condition=%wide.region_11.13_spmd.clone.clone.clone, body=%wide.region_10.12_spmd.sunk.clone.clone.clone.sunk | while | flops 70322144 | bytes 2021583 | solution.py:156
  70.3 0.6 gather_fusion.2
  70.9 0.6 gather_fusion.3
  71.5 0.4 fusion.248
  72.0 0.7 gather_fusion
  73.0 0.8 gather_fusion.5
  74.0 0.8 gather_fusion.4
  74.8 0.7 gather_fusion.1
  75.5 0.7 gather_fusion.6
  76.2 0.6 add_compare_fusion.6
  76.8 14.2 %fusion.249 = f32[2,64,128]{2,0,1:T(2,128)S(1)} fusion(f32[64,128]{1,0:T(8,128)S(1)} %bitcast.216, f32[64,128]{1,0:T(8,128)S(1)} %bitcast.222, f32[64,128]{1,0:T(8,128)S(1)} %bitcast.220, f32[64,128]{1,0:T(8,128)S(1)} %broadcast_add_fusion.19, f32[64,128]{1,0:T(8,128)S(1)} %bitcast.221, f32[64,128]{1,0:T(8,128)S(1)} %broadcast_add_fusion.20, ...), kind=kOutput, calls=%fused_computation.77.clone.1 | convolution fusion | flops 57671680 | bytes 409728 | tf_op jit(solution)/shard_map/while/body/gij,kgi->kgj/dot_general | solution.py:150
  91.3 37.4 %all_to_all.68 = f32[32,2,256]{2,1,0:T(2,128)S(1)} all-to-all(f32[32,2,256]{2,1,0:T(2,128)S(1)} %copy.39), channel_id=1, replica_groups=mesh['row_0'=8,'row_1'=2,'col_0'=8,'col_1'=4] {'col_0','col_1'}, dimensions={0} | all-to-all | bytes 131072 | tf_op jit(solution)/shard_map/all_to_all | solution.py:63
  129.0 14.0 %all_to_all.69 = f32[64,1,4]{2,1,0:T(1,128)S(1)} all-to-all(f32[64,1,4]{2,1,0:T(1,128)S(1)} %broadcast_in_dim.295), channel_id=1, replica_groups=mesh['row_0'=8,'row_1'=2,'col_0'=8,'col_1'=4] {'row_1','col_0','col_1'}, dimensions={0} | all-to-all | bytes 2048 | tf_op jit(solution)/shard_map/all_to_all | solution.py:23
  143.0 0.6 broadcast_in_dim.296
  143.6 4.2 %all-to-all-start.3 = ((f32[8,1,4]{2,1,0:T(1,128)}), f32[8,1,4]{2,1,0:T(1,128)S(1)}, u32[]{:S(2)}, u32[]{:S(2)}) async-start(f32[8,1,4]{2,1,0:T(1,128)} %broadcast_in_dim.296), calls=%async_computation.3 | async-start | bytes 8192 | tf_op jit(solution)/shard_map/all_to_all | solution.py:23
  147.9 6.6 %all-to-all-done.3 = f32[8,1,4]{2,1,0:T(1,128)S(1)} async-done(((f32[8,1,4]{2,1,0:T(1,128)}), f32[8,1,4]{2,1,0:T(1,128)S(1)}, u32[]{:S(2)}, u32[]{:S(2)}) %all-to-all-start.3) | async-done | bytes 160 | tf_op jit(solution)/shard_map/all_to_all | solution.py:23
  154.6 16.5 %all_gather.14 = f32[2,4096]{1,0:T(2,128)S(1)} all-gather(f32[2,256]{1,0:T(2,128)S(1)} %multiply_subtract_fusion.1), channel_id=1, replica_groups=mesh['row_0'=8,'row_1'=2,'col_0'=8,'col_1'=4] {'row_0','row_1'}, dimensions={1}, use_global_device_ids=true | all-gather | bytes 34816 | tf_op jit(solution)/shard_map/all_gather | solution.py:146
  171.2 21.0 %while.49 = (s32[]{:T(128)}, f32[2,64,128]{2,1,0:T(8,128)S(1)}, s32[]{:T(128)}, s32[2112]{0:T(1024)S(1)}, f32[2,32,128]{2,0,1:T(2,128)S(1)}, /*index=5*/s32[]{:T...) while((s32[]{:T(128)}, f32[2,64,128]{2,1,0:T(8,128)S(1)}, ...), condition=%wide.region_19.21_spmd.clone.clone.clone, body=%wide.region_18.20_spmd.sunk.clone.clone.clone.sunk | while | flops 70322144 | bytes 2021583 | solution.py:156
  171.3 0.6 gather_fusion.9
  171.9 0.6 gather_fusion.10
  172.5 0.4 fusion.257
  173.0 0.7 gather_fusion.7
  174.0 0.8 gather_fusion.12
  175.0 0.8 gather_fusion.11
  175.8 0.7 gather_fusion.8
  176.5 0.7 gather_fusion.13
  177.2 0.6 add_compare_fusion.7
  177.8 14.2 %fusion.258 = f32[2,64,128]{2,0,1:T(2,128)S(1)} fusion(f32[64,128]{1,0:T(8,128)S(1)} %bitcast.217, f32[64,128]{1,0:T(8,128)S(1)} %bitcast.226, f32[64,128]{1,0:T(8,128)S(1)} %bitcast.224, f32[64,128]{1,0:T(8,128)S(1)} %broadcast_add_fusion.22, f32[64,128]{1,0:T(8,128)S(1)} %bitcast.225, f32[64,128]{1,0:T(8,128)S(1)} %broadcast_add_fusion.23, ...), kind=kOutput, calls=%fused_computation.161.clone.1 | convolution fusion | flops 57671680 | bytes 409728 | tf_op jit(solution)/shard_map/while/body/gij,kgi->kgj/dot_general | solution.py:150
  192.3 32.5 %all_to_all.70 = f32[32,2,256]{2,1,0:T(2,128)S(1)} all-to-all(f32[32,2,256]{2,1,0:T(2,128)S(1)} %copy.42), channel_id=1, replica_groups=mesh['row_0'=8,'row_1'=2,'col_0'=8,'col_1'=4] {'col_0','col_1'}, dimensions={0} | all-to-all | bytes 131072 | tf_op jit(solution)/shard_map/all_to_all | solution.py:63
  225.1 14.2 %all_to_all.71 = f32[64,1,4]{2,1,0:T(1,128)S(1)} all-to-all(f32[64,1,4]{2,1,0:T(1,128)S(1)} %broadcast_in_dim.297), channel_id=1, replica_groups=mesh['row_0'=8,'row_1'=2,'col_0'=8,'col_1'=4] {'row_1','col_0','col_1'}, dimensions={0} | all-to-all | bytes 2048 | tf_op jit(solution)/shard_map/all_to_all | solution.py:23
  239.4 0.6 broadcast_in_dim.298
  240.0 3.5 all-to-all-start.6
  243.5 6.6 %all-to-all-done.6 = f32[8,1,4]{2,1,0:T(1,128)S(1)} async-done(((f32[8,1,4]{2,1,0:T(1,128)}), f32[8,1,4]{2,1,0:T(1,128)S(1)}, u32[]{:S(2)}, u32[]{:S(2)}) %all-to-all-start.6) | async-done | bytes 160 | tf_op jit(solution)/shard_map/all_to_all | solution.py:23
  250.2 16.5 %all_gather.15 = f32[2,4096]{1,0:T(2,128)S(1)} all-gather(f32[2,256]{1,0:T(2,128)S(1)} %multiply_subtract_fusion), channel_id=1, replica_groups=mesh['row_0'=8,'row_1'=2,'col_0'=8,'col_1'=4] {'row_0','row_1'}, dimensions={1}, use_global_device_ids=true | all-gather | bytes 34816 | tf_op jit(solution)/shard_map/all_gather | solution.py:146
  266.8 21.0 %while.50 = (s32[]{:T(128)}, f32[2,64,128]{2,1,0:T(8,128)S(1)}, s32[]{:T(128)}, s32[2112]{0:T(1024)S(1)}, f32[2,32,128]{2,0,1:T(2,128)S(1)}, /*index=5*/s32[]{:T...) while((s32[]{:T(128)}, f32[2,64,128]{2,1,0:T(8,128)S(1)}, ...), condition=%wide.region_26.28_spmd.clone.clone.clone, body=%wide.region_25.27_spmd.sunk.clone.clone.clone.sunk | while | flops 70322144 | bytes 2021583 | solution.py:156
  266.9 0.6 gather_fusion.16
  267.5 0.6 gather_fusion.17
  268.1 0.4 fusion.266
  268.6 0.7 gather_fusion.14
  269.6 0.8 gather_fusion.19
  270.6 0.8 gather_fusion.18
  271.4 0.7 gather_fusion.15
  272.1 0.7 gather_fusion.20
  272.8 0.6 add_compare_fusion.8
  273.4 14.2 %fusion.267 = f32[2,64,128]{2,0,1:T(2,128)S(1)} fusion(f32[64,128]{1,0:T(8,128)S(1)} %bitcast.218, f32[64,128]{1,0:T(8,128)S(1)} %bitcast.230, f32[64,128]{1,0:T(8,128)S(1)} %bitcast.228, f32[64,128]{1,0:T(8,128)S(1)} %broadcast_add_fusion.25, f32[64,128]{1,0:T(8,128)S(1)} %bitcast.229, f32[64,128]{1,0:T(8,128)S(1)} %broadcast_add_fusion.26, ...), kind=kOutput, calls=%fused_computation.245.clone.1 | convolution fusion | flops 57671680 | bytes 409728 | tf_op jit(solution)/shard_map/while/body/gij,kgi->kgj/dot_general | solution.py:150
  287.9 32.5 %all_to_all.72 = f32[32,2,256]{2,1,0:T(2,128)S(1)} all-to-all(f32[32,2,256]{2,1,0:T(2,128)S(1)} %copy.45), channel_id=1, replica_groups=mesh['row_0'=8,'row_1'=2,'col_0'=8,'col_1'=4] {'col_0','col_1'}, dimensions={0} | all-to-all | bytes 131072 | tf_op jit(solution)/shard_map/all_to_all | solution.py:63
  320.7 14.2 %all_to_all.73 = f32[64,1,4]{2,1,0:T(1,128)S(1)} all-to-all(f32[64,1,4]{2,1,0:T(1,128)S(1)} %broadcast_in_dim.299), channel_id=1, replica_groups=mesh['row_0'=8,'row_1'=2,'col_0'=8,'col_1'=4] {'row_1','col_0','col_1'}, dimensions={0} | all-to-all | bytes 2048 | tf_op jit(solution)/shard_map/all_to_all | solution.py:23
  335.0 9.8 %all_to_all.74 = f32[8,1,4]{2,1,0:T(1,128)S(1)} all-to-all(f32[8,1,4]{2,1,0:T(1,128)S(1)} %broadcast_in_dim.300), channel_id=1, replica_groups=mesh['row_0'=8,'row_1'=2,'col_0'=8,'col_1'=4] {'row_0'}, dimensions={0} | all-to-all | bytes 256 | tf_op jit(solution)/shard_map/all_to_all | solution.py:23
  345.2 14.5 %all_to_all.75 = f32[64,1,2]{2,1,0:T(1,128)S(1)} all-to-all(f32[64,1,2]{2,1,0:T(1,128)S(1)} %broadcast_in_dim.301), channel_id=1, replica_groups=mesh['row_0'=8,'row_1'=2,'col_0'=8,'col_1'=4] {'row_1','col_0','col_1'}, dimensions={0} | all-to-all | bytes 1024 | tf_op jit(solution)/shard_map/all_to_all | solution.py:23
  359.8 8.9 %all_to_all.76 = f32[8,1,2]{2,1,0:T(1,128)S(1)} all-to-all(f32[8,1,2]{2,1,0:T(1,128)S(1)} %broadcast_in_dim.302), channel_id=1, replica_groups=mesh['row_0'=8,'row_1'=2,'col_0'=8,'col_1'=4] {'row_0'}, dimensions={0} | all-to-all | bytes 128 | tf_op jit(solution)/shard_map/all_to_all | solution.py:23
  368.8 0.6 fusion.214
  370.7 0.6 fusion.204
  (120 shorter events, 7.1 us)
Async XLA Ops:
  0.0 18.2 %copy-start.3 = (s32[3,1024]{1,0:T(4,128)S(1)}, s32[3,1024]{1,0:T(4,128)}, u32[]{:S(2)}) copy-start(s32[3,1024]{1,0:T(4,128)} %param.17) | copy-start | bytes 36868
  2.2 67.9 %all-to-all-start = ((f32[32,4,256]{2,1,0:T(4,128)}), f32[32,4,256]{2,1,0:T(4,128)S(1)}, u32[]{:S(2)}, u32[]{:S(2)}) async-start(f32[32,4,256]{2,1,0:T(4,128)} %broadcast_in_dim.293), calls=%async_computation | async-start | bytes 262144 | tf_op jit(solution)/shard_map/all_to_all | solution.py:23
  18.2 51.9 %copy-start = (s32[3]{0:T(128)S(1)}, s32[3]{0:T(128)}, u32[]{:S(2)}) copy-start(s32[3]{0:T(128)} %constant.962) | copy-start | bytes 40
  18.2 51.9 %copy-start.1 = (s32[3]{0:T(128)S(1)}, s32[3]{0:T(128)}, u32[]{:S(2)}) copy-start(s32[3]{0:T(128)} %constant.963) | copy-start | bytes 40
  18.2 51.9 %copy-start.2 = (s32[3]{0:T(128)S(1)}, s32[3]{0:T(128)}, u32[]{:S(2)}) copy-start(s32[3]{0:T(128)} %constant.964) | copy-start | bytes 40
  143.6 10.8 %all-to-all-start.3 = ((f32[8,1,4]{2,1,0:T(1,128)}), f32[8,1,4]{2,1,0:T(1,128)S(1)}, u32[]{:S(2)}, u32[]{:S(2)}) async-start(f32[8,1,4]{2,1,0:T(1,128)} %broadcast_in_dim.296), calls=%async_computation.3 | async-start | bytes 8192 | tf_op jit(solution)/shard_map/all_to_all | solution.py:23
  240.0 10.1 %all-to-all-start.6 = ((f32[8,1,4]{2,1,0:T(1,128)}), f32[8,1,4]{2,1,0:T(1,128)S(1)}, u32[]{:S(2)}, u32[]{:S(2)}) async-start(f32[8,1,4]{2,1,0:T(1,128)} %broadcast_in_dim.298), calls=%async_computation.6 | async-start | bytes 8192 | tf_op jit(solution)/shard_map/all_to_all | solution.py:23
where the time goes:
time: 372 us; the launch traced here: 371 us
  blocking collectives  245 us (66%)
  matrix products  43.2 us (12%)
  other arithmetic  25.8 us (7%)
  starting transfers between devices  21.4 us (6%)
  local copies, waits for them, and re-layouts  20.5 us (6%)
  waiting for transfers between devices  13.1 us (4%)
    all_to_all x3, blocking collectives, sent_and_summed(): lax.all_to_all(in_blocks(value, dim, devices), axis, 0, 0, tiled=True)  102 us
    all_to_all x6, blocking collectives, copy_for_each(): lax.all_to_all(jnp.broadcast_to(value[None], (devices, *value.shape)), ax...  75.7 us
    all_gather x3, blocking collectives, apply(): lax.all_gather(direction, ROW, axis=1, tiled=True).reshape(2, n_tgt, BLOCK)  51.5 us
    dot_general x3, matrix products, turn(): jnp.einsum('gij,kgi->kgj', kern, remote[:, tgt_blk], precision=lax.Precis...  42.6 us
    all_to_all x3, starting transfers between devices, copy_for_each(): lax.all_to_all(jnp.broadcast_to(value[None], (devices, *value.shape)), ax...  21.4 us
    all_gather x1, blocking collectives, per_device(): lax.all_gather(geo, ROW, axis=1, tiled=True).reshape(4, n_tgt, BLOCK)  15.1 us
    scatter-add x1, other arithmetic, per_device(): jnp.nonzero(tile, size=n_tgt * n_src + pair_group, fill_value=0)[0]  14.7 us
    all_to_all x3, waiting for transfers between devices, copy_for_each(): lax.all_to_all(jnp.broadcast_to(value[None], (devices, *value.shape)), ax...  13.1 us
  transfers between devices with their start and end apart: 3, of which 2 were waited for; matrix products, arithmetic and copies ran while one was open for 5% of the time, Pallas kernels for 0%

commit v1 on v0

v1 whole, which is shorter than its diff:
```python
import jax
import jax.numpy as jnp
from jax import lax
from jax.experimental import pallas as pl
from jax.experimental.pallas import tpu as pltpu
from jax.sharding import Mesh
from jax.sharding import PartitionSpec as P

LANES = 128
NX, NY, NZ, NQ = 4, 8, 8, 16
OWN = 17
PAIRS = 27
SLOTS = 36
MOMENTS = 10
SHIFTS = (200.0, 20.0)
F32 = jnp.float32
AXES = ("y", "c", "z", "x")
HIGH = lax.Precision.HIGHEST
HALO = [(a, b, d) for a in (-1, 0, 1) for b in (-1, 0, 1) for d in (-1, 0, 1) if (a, b, d) != (0, 0, 0)]


def far_first(n):
    return sorted(range(1, n), key=lambda k: -min(k, n - k))


def choose(kind, table):
    low = jnp.where(kind < 0.5, table[0], table[1])
    high = jnp.where(kind < 2.5, table[2], table[3])
    return jnp.where(kind < 1.5, low, high)


class Exchange:
    def __init__(self, peers, send, recv):
        self.peers, self.send, self.recv = peers, send, recv
        self.copies = []

    def start(self, src, dst):
        self.copies = []
        for k, peer in self.peers:
            copy = pltpu.make_async_remote_copy(
                src_ref=src(k),
                dst_ref=dst(k),
                send_sem=self.send.at[k],
                recv_sem=self.recv.at[k],
                device_id=peer,
                device_id_type=pl.DeviceIdType.MESH,
            )
            copy.start()
            self.copies.append(copy)

    def wait(self):
        for copy in self.copies:
            copy.wait_recv()

    def finish(self):
        for copy in self.copies:
            copy.wait_send()


def kernel(
    idx, chi_t, eta_t, gam_t, off, typ, out,
    gat, sel, rcv, hal, feat, tgt, hbuf, hv0, hv1, hv2,
    rgat, rsel, rrcv, own0, az, ax, aq, msgs,
    zs, zr, xs, xr, qs, qr, hs, hr, h1s, h1r, h2s, h2r,
    rzs, rzr, rxs, rxr, rqs, rqr, dzs, dzr, dxs, dxr, dqs, dqr,
):
    my = lax.axis_index("y")
    mc = lax.axis_index("c")
    mz = lax.axis_index("z")
    mx = lax.axis_index("x")
    mq = my * 2 + mc
    gx = mz * 2 + mc
    zpeers = [(k, {"z": lax.rem(mz + k, NZ)}) for k in far_first(NZ)]
    xpeers = [(k, {"x": lax.rem(mx + k, NX)}) for k in far_first(NX)]
    qpeers = []
    for k in sorted(range(1, NQ), key=lambda k: -min(k, NQ - k)):
        q = lax.rem(mq + k, NQ)
        qpeers.append((k, {"y": q // 2, "c": lax.rem(q, 2)}))
    hpeers = []
    for k, (ex, ez, ey) in enumerate(HALO):
        g = lax.rem(gx + ex + 16, 16)
        hpeers.append((k, {
            "z": g // 2, "c": lax.rem(g, 2),
            "x": lax.rem(mx + ez + NX, NX), "y": lax.rem(my + ey + NY, NY),
        }))

    barrier = pltpu.get_barrier_semaphore()
    everyone = zpeers + xpeers + qpeers + hpeers
    for _, peer in everyone:
        pl.semaphore_signal(barrier, inc=1, device_id=peer, device_id_type=pl.DeviceIdType.MESH)

    for b in range(2):
        lanes = pl.ds(b * LANES, LANES)
        kind = typ[b : b + 1, :].astype(F32)
        for comp in range(3):
            gat[mx, mz, b, comp : comp + 1, :] = off[comp : comp + 1, lanes]
        gat[mx, mz, b, 3:4, :] = kind
        own0[b, 0:1, :] = -choose(kind, chi_t)
        own0[b, 1:2, :] = jnp.full((1, LANES), -1.0, F32)
    pl.semaphore_wait(barrier, len(everyone))

    def half(k):
        return (0, 2) if HALO[k][2] == 0 else ((1, 1) if HALO[k][2] == 1 else (0, 1))

    def halo_src(ref):
        return lambda k: ref.at[pl.ds(OWN + half(k)[0], half(k)[1])]

    def halo_dst(ref):
        def at(k):
            ex, ez, ey = HALO[k]
            first, n = half(k)
            slot = ((1 - ex) * 3 + (1 - ez)) * 4 + first + 1 - 2 * ey
            return ref.at[pl.ds(slot, n)]
        return at

    zg = Exchange(zpeers, zs, zr)
    zg.start(lambda k: gat.at[mx, mz], lambda k: gat.at[mx, mz])
    zg.wait()
    xg = Exchange(xpeers, xs, xr)
    xg.start(lambda k: gat.at[mx], lambda k: gat.at[mx])
    xg.wait()

    def to_q(q, base, source, chosen):
        for s in range(2):
            i = idx[base + q * 2 + s]
            chosen[q, s] = source[i // 16, lax.rem(i, 16) // 2, lax.rem(i, 2)]

    def pick_all(base, source, chosen, received):
        def one(q, carry):
            to_q(q, base, source, chosen)
            return carry
        lax.fori_loop(0, NQ, one, 0, unroll=True)
        for s in range(2):
            i = idx[base + mq * 2 + s]
            received[mq, s] = source[i // 16, lax.rem(i, 16) // 2, lax.rem(i, 2)]

    pick_all(0, gat, sel, rcv)
    qg = Exchange(qpeers, qs, qr)
    qg.start(lambda k: sel.at[lax.rem(mq + k, NQ)], lambda k: rcv.at[mq])
    qg.wait()
    for s in range(2):
        hal[OWN + s] = rcv[idx[64 + s], s]
    hg = Exchange(hpeers, hs, hr)
    hg.start(halo_src(hal), halo_dst(hal))

    comp = lax.broadcasted_iota(jnp.int32, (4, LANES), 0)

    def features(slot):
        raw = hal[slot]
        sx = (slot // 12 - 1) * 11
        sz = (lax.rem(slot, 12) // 4 - 1) * 11
        sy = (lax.rem(slot, 4) - 1) * 11
        shift = jnp.where(comp == 0, sx, jnp.where(comp == 1, sy, sz)).astype(F32)
        kind = hal[slot, 3:4, :]
        gam = choose(kind, gam_t)
        shield = (lax.rsqrt(gam) / gam) * (0.001 ** 0.5)
        feat[slot] = jnp.where(comp == 3, jnp.broadcast_to(shield, (4, LANES)), (raw + shift) * 0.1)
        hv0[slot, 0:1, :] = -choose(kind, chi_t)
        hv0[slot, 1:2, :] = jnp.full((1, LANES), -1.0, F32)

    for t in range(2):
        features(OWN + t)
        for c in range(4):
            tgt[t, c] = jnp.broadcast_to(feat[OWN + t, c : c + 1, :], (LANES, LANES)).T

    hg.wait()

    def all_features(slot, carry):
        features(slot)
        return carry
    lax.fori_loop(0, SLOTS, all_features, 0)

    for t in range(2):
        def one_pair(n, carry):
            slot = (n // 3) * 4 + lax.rem(n, 3) + t
            src = [feat[slot, c : c + 1, :] for c in range(4)]
            for j in range(16):
                rows = pl.ds(j * 8, 8)
                dx = src[0] - tgt[t, 0, rows, :]
                dy = src[1] - tgt[t, 1, rows, :]
                dz = src[2] - tgt[t, 2, rows, :]
                r2 = jnp.maximum(dx * dx + dy * dy + dz * dz, 1e-30)
                r = r2 * lax.rsqrt(r2)
                cube = r2 * r + src[3] * tgt[t, 3, rows, :]
                inv = jnp.exp2(jnp.log2(cube) * (-1.0 / 3.0))
                u = jnp.maximum(1.0 - r, 0.0)
                u = u * u
                poly = ((28.8 * r + 14.4) * r + 5.76) * r + 1.44
                hbuf[t, n, rows, :] = (u * u) * poly * inv
            return carry
        lax.fori_loop(0, PAIRS, one_pair, 0)
        eta = choose(hal[OWN + t, 3:4, :], eta_t)
        diag = lax.broadcasted_iota(jnp.int32, (LANES, LANES), 0) == lax.broadcasted_iota(jnp.int32, (LANES, LANES), 1)
        hbuf[t, 13] = jnp.where(diag, eta, hbuf[t, 13])

    ones = jnp.ones((8, LANES), F32)
    rhs_row = lax.broadcasted_iota(jnp.int32, (2, LANES), 0)

    def matvec(vec):
        res = []
        for t in range(2):
            def near(n, carry):
                acc_s, acc_t = carry
                for d in range(3):
                    h = hbuf[t, n * 3 + d]
                    v = vec[n * 4 + d + t]
                    acc_s = acc_s + h * v[0:1, :]
                    acc_t = acc_t + h * v[1:2, :]
                return acc_s, acc_t
            zero = jnp.zeros((LANES, LANES), F32)
            acc_s, acc_t = lax.fori_loop(0, 9, near, (zero, zero))
            dims = (((1,), (1,)), ((), ()))
            sum_s = lax.dot_general(ones, acc_s, dims, precision=HIGH, preferred_element_type=F32)
            sum_t = lax.dot_general(ones, acc_t, dims, precision=HIGH, preferred_element_type=F32)
            res.append(jnp.where(rhs_row == 0, sum_s[0:2], sum_t[0:2]))
        return res

    v1 = matvec(hv0)
    for t in range(2):
        hv1[OWN + t] = v1[t] - SHIFTS[0] * hv0[OWN + t]
    g1 = Exchange(hpeers, h1s, h1r)
    g1.start(halo_src(hv1), halo_dst(hv1))
    g1.wait()
    v2 = matvec(hv1)
    for t in range(2):
        hv2[OWN + t] = v2[t] - SHIFTS[1] * hv1[OWN + t]
    g2 = Exchange(hpeers, h2s, h2r)
    g2.start(halo_src(hv2), halo_dst(hv2))
    for t in range(2):
        rgat[mx, mz, t, 0:2, :] = hv1[OWN + t]
        rgat[mx, mz, t, 2:4, :] = hv2[OWN + t]
    rz = Exchange(zpeers, rzs, rzr)
    rz.start(lambda k: rgat.at[mx, mz], lambda k: rgat.at[mx, mz])
    g2.wait()
    v3 = matvec(hv2)

    lane = lax.broadcasted_iota(jnp.int32, (2, LANES), 1)
    v = [[hv0[OWN + t] for t in range(2)], [hv1[OWN + t] for t in range(2)], [hv2[OWN + t] for t in range(2)], v3]
    terms = [v[a][0] * v[b][0] + v[a][1] * v[b][1] for a, b in ((0, 0), (0, 1), (0, 2), (1, 1), (1, 2), (2, 2), (2, 3))]
    terms += [v[a][0] + v[a][1] for a in range(3)]
    msg = jnp.zeros((2, LANES), F32)
    for k, term in enumerate(terms):
        msg = jnp.where(lane == k, jnp.sum(term, axis=1, keepdims=True), msg)
    msgs[0] = msg
    az[mz] = msg
    dz_ = Exchange(zpeers, dzs, dzr)
    dz_.start(lambda k: msgs.at[0], lambda k: az.at[mz])
    rz.wait()
    rx = Exchange(xpeers, rxs, rxr)
    rx.start(lambda k: rgat.at[mx], lambda k: rgat.at[mx])
    dz_.wait()
    msg = az[0]
    for k in range(1, NZ):
        msg = msg + az[k]
    msgs[1] = msg
    ax[mx] = msg
    dx_ = Exchange(xpeers, dxs, dxr)
    dx_.start(lambda k: msgs.at[1], lambda k: ax.at[mx])
    rx.wait()
    pick_all(32 + 34, rgat, rsel, rrcv)
    rq = Exchange(qpeers, rqs, rqr)
    rq.start(lambda k: rsel.at[lax.rem(mq + k, NQ)], lambda k: rrcv.at[mq])
    dx_.wait()
    msg = ax[0]
    for k in range(1, NX):
        msg = msg + ax[k]
    msgs[2] = msg
    aq[mq] = msg
    dq_ = Exchange(qpeers, dqs, dqr)
    dq_.start(lambda k: msgs.at[2], lambda k: aq.at[mq])
    rq.wait()
    back = [rrcv[idx[130 + s], s] for s in range(2)]
    dq_.wait()
    msg = aq[0]
    for k in range(1, NQ):
        msg = msg + aq[k]

    m = [jnp.broadcast_to(msg[:, k : k + 1], (2, LANES)) for k in range(MOMENTS)]
    gram = {(0, 0): m[0], (0, 1): m[1], (0, 2): m[2], (1, 1): m[3], (1, 2): m[4], (2, 2): m[5]}
    sums = m[7:]

    def dot(i, j):
        return gram[min(i, j), max(i, j)]

    def image_dot(i, j):
        i, j = min(i, j), max(i, j)
        return m[6] if i == 2 else dot(i + 1, j) + SHIFTS[i] * dot(i, j)

    def quadratic(a, form):
        total = None
        for i, ai in enumerate(a):
            for j in range(i, len(a)):
                term = ai * a[j] * form(i, j)
                term = term if i == j else term + term
                total = term if total is None else total + term
        return total

    def image(a):
        res = [None] * (len(a) + 1)
        for i, ai in enumerate(a):
            res[i + 1] = ai
            res[i] = SHIFTS[i] * ai if res[i] is None else res[i] + SHIFTS[i] * ai
        return res

    def plus(a, scale, b):
        res = []
        for i in range(max(len(a), len(b))):
            ai = a[i] if i < len(a) else None
            bi = b[i] if i < len(b) else None
            if bi is None:
                res.append(ai)
            elif ai is None:
                res.append(scale * bi)
            else:
                res.append(ai + scale * bi)
        return res

    one = jnp.ones((2, LANES), F32)
    x, r, p = [], [one], [one]
    rr = m[0]
    for step in range(3):
        alpha = rr / quadratic(p, image_dot)
        x = plus(x, alpha, p)
        if step < 2:
            r = plus(r, -alpha, image(p))
            new = quadratic(r, dot)
            p = plus(r, new / rr, p)
            rr = new
    total = x[0] * sums[0] + x[1] * sums[1] + x[2] * sums[2]
    ratio = total[0:1] / total[1:2]
    for s in range(2):
        b = back[s]
        part = x[0] * own0[s] + x[1] * b[0:2] + x[2] * b[2:4]
        out[s : s + 1, :] = part[0:1] - ratio * part[1:2]

    for e in (zg, xg, qg, hg, g1, g2, rz, rx, rq, dz_, dx_, dq_):
        e.finish()


def place(cell):
    return cell[2] * 8 + cell[0] // 2, cell[1] % 2, (cell[1] // 2) * 2 + cell[0] % 2


def per_device(offsets, cells, types, mask, chi_table, eta_table, gamma_table):
    my, mc = lax.axis_index("y"), lax.axis_index("c")
    mz, mx = lax.axis_index("z"), lax.axis_index("x")
    mq = my * 2 + mc
    col = mz * 4 + mx
    nb = cells.shape[1]
    key = (cells[0] * 16 + cells[1]) * 4 + cells[2]
    q = jnp.arange(32, dtype=jnp.int32) // 2
    s = jnp.arange(32, dtype=jnp.int32) % 2

    def target(q, s):
        return ((2 * mz + q % 2) * 16 + 2 * (q // 2) + s) * 4 + mx

    two = jnp.arange(2, dtype=jnp.int32)
    wanted = jnp.concatenate([target(q, s), target(mq, two)])
    ids = jnp.arange(nb, dtype=jnp.int32)
    block = jnp.sum(jnp.where(key[None, :] == wanted[:, None], ids[None, :], 0), axis=1).astype(jnp.int32)
    local = block % 64
    at = local // 2
    fwd = ((at % 4) * 8 + at // 4) * 2 + local % 2
    fwd_owner = block // 64
    mine = jnp.concatenate([q * 64 + col * 2 + s, mq * 64 + col * 2 + two])
    cell = jnp.take(cells, mine, axis=1)
    spot, slot, holder = place(cell)
    rev = spot * 2 + slot
    idx = jnp.concatenate([
        fwd[:32], jnp.zeros((32,), jnp.int32), fwd_owner[32:], rev[:32], jnp.zeros((32,), jnp.int32), holder[32:],
    ])

    def vmem(*shape):
        return pltpu.VMEM(shape, F32)

    def sems(n):
        return [pltpu.SemaphoreType.DMA((n,)), pltpu.SemaphoreType.DMA((n,))]

    smem = pl.BlockSpec(memory_space=pltpu.SMEM)
    whole = pl.BlockSpec(memory_space=pltpu.VMEM)
    charges = pl.pallas_call(
        kernel,
        out_shape=jax.ShapeDtypeStruct((2, LANES), F32),
        in_specs=[smem] * 4 + [whole] * 2,
        out_specs=whole,
        scratch_shapes=[
            vmem(NX, NZ, 2, 4, LANES), vmem(NQ, 2, 4, LANES), vmem(NQ, 2, 4, LANES),
            vmem(SLOTS, 4, LANES), vmem(SLOTS, 4, LANES), vmem(2, 4, LANES, LANES),
            vmem(2, PAIRS, LANES, LANES),
            vmem(SLOTS, 2, LANES), vmem(SLOTS, 2, LANES), vmem(SLOTS, 2, LANES),
            vmem(NX, NZ, 2, 4, LANES), vmem(NQ, 2, 4, LANES), vmem(NQ, 2, 4, LANES),
            vmem(2, 2, LANES), vmem(NZ, 2, LANES), vmem(NX, 2, LANES), vmem(NQ, 2, LANES), vmem(3, 2, LANES),
            *sems(NZ), *sems(NX), *sems(NQ), *sems(26), *sems(26), *sems(26),
            *sems(NZ), *sems(NX), *sems(NQ), *sems(NZ), *sems(NX), *sems(NQ),
        ],
        compiler_params=pltpu.CompilerParams(collective_id=0, has_side_effects=True),
    )(idx, chi_table, eta_table, gamma_table, offsets, types.reshape(2, LANES))
    return charges.reshape(2 * LANES)


def solution(mesh):
    torus = Mesh(mesh.devices.reshape(8, 2, 8, 4), AXES)
    placed = (P(None, AXES), P(), P(AXES), P(None, ("z", "x"), ("y", "c"), None), P(), P(), P())
    return jax.shard_map(
        per_device, mesh=torus, in_specs=placed, out_specs=P(AXES), check_vma=False
    )
```

time: 372 us -> 74.4 us (0.20)
  blocking collectives: 245 us -> 0 us
  Pallas kernels: 0 us -> 70 us
  matrix products: 43.2 us -> 0 us
  other arithmetic: 25.8 us -> 0.83 us
  starting transfers between devices: 21.4 us -> 0 us
  local copies, waits for them, and re-layouts: 20.5 us -> 3.25 us
  waiting for transfers between devices: 13.1 us -> 0 us
    all_to_all x9 -> x0, blocking collectives: 178 us -> none  [the longest x3 102 us: sent_and_summed(): lax.all_to_all(in_blocks(value, dim, devices), axis, 0, 0, tiled=True)]
    pallas_call x0 -> x1, Pallas kernels: none -> 70 us  [per_device(): pl.pallas_call(kernel, out_shape=jax.ShapeDtypeStruct((2, LANES), F32), i...]
    all_gather x4 -> x0, blocking collectives: 66.6 us -> none  [the longest x3 51.5 us: apply(): lax.all_gather(direction, ROW, axis=1, tiled=True).reshape(2, n_tgt, BLOCK)]
    dot_general x6 -> x0, matrix products: 43.2 us -> none  [the longest x3 42.6 us: turn(): jnp.einsum('gij,kgi->kgj', kern, remote[:, tgt_blk], precision=lax.Precis...]
    all_to_all x3 -> x0, starting transfers between devices: 21.4 us -> none  [copy_for_each(): lax.all_to_all(jnp.broadcast_to(value[None], (devices, *value.shape)), ax...]
    gather x23 -> x1, local copies, waits for them, and re-layouts: 15.4 us -> 0.58 us  [per_device(): cell = jnp.take(cells, mine, axis=1)]
    scatter-add x1 -> x0, other arithmetic: 14.7 us -> none  [per_device(): jnp.nonzero(tile, size=n_tgt * n_src + pair_group, fill_value=0)[0]]
    all_to_all x3 -> x0, waiting for transfers between devices: 13.1 us -> none  [copy_for_each(): lax.all_to_all(jnp.broadcast_to(value[None], (devices, *value.shape)), ax...]
  transfers between devices with their start and end apart: 3 -> 0, of which waited for: 2 -> 0; matrix products, arithmetic and copies ran while one was open for 5% -> 0% of each run, Pallas kernels for 0% -> 0%
where the time goes in v1:
time: 74.4 us; the launch traced here: 74.2 us
  Pallas kernels  70 us (94%)
  local copies, waits for them, and re-layouts  3.25 us (4%)
  other arithmetic  0.83 us (1%)
    pallas_call x1, Pallas kernels, per_device(): pl.pallas_call(kernel, out_shape=jax.ShapeDtypeStruct((2, LANES), F32), i...  70 us
    unnamed x6, local copies, waits for them, and re-layouts  1.88 us

profile of v1, /device:TPU:1, one launch (start us, length us, event | category | flops | bytes accessed | tf_op | source)
XLA Modules:
  0.0 74.2 jit_solution(14379497873423328408)
XLA Ops:
  0.0 0.0 copy-start
  0.0 0.1 pad_add_fusion
  0.1 0.1 fusion.10
  0.2 0.1 compare_and_fusion
  0.3 0.4 copy-done
  0.7 0.2 select_reduce_fusion
  1.0 0.1 slice.36
  1.0 0.2 copy.9
  1.3 0.6 gather_fusion
  1.8 0.1 select_bitcast_fusion
  1.9 0.2 slice_reduce_fusion
  2.2 0.1 slice.41
  2.2 0.7 concatenate.41.idx
  2.9 70.0 %shard_map.64 = f32[2,128]{1,0:T(2,128)} custom-call(s32[132]{0:T(256)} %concatenate.41.idx, f32[4]{0:T(128)} %chi_t.1, f32[4]{0:T(128)} %eta_t.1, f32[4]{0:T(128)} %gam_t.1, f32[3,256]{1,0:T(4,128)} %off.1, s32[2,128]{1,0:T(2,128)} %bitcast.16), custom_call_target="tpu_custom_call" | custom-call | tf_op jit(solution)/shard_map/pallas_call | solution.py:381
  72.9 0.0 copy-start.1
  72.9 0.7 copy-done.1
  73.6 0.6 copy.11
  (11 shorter events, 0.1 us)
Async XLA Ops:
  0.0 0.7 copy-start
  72.9 0.7 copy-start.1

commit v2 on v1

v2 whole, which is shorter than its diff:
```python
import jax
import jax.numpy as jnp
from jax import lax
from jax.experimental import pallas as pl
from jax.experimental.pallas import tpu as pltpu
from jax.sharding import Mesh
from jax.sharding import PartitionSpec as P

LANES = 128
NX, NY, NZ, NQ = 4, 8, 8, 16
OWN = 17
PAIRS = 27
SLOTS = 36
MOMENTS = 10
SHIFTS = (200.0, 20.0)
F32 = jnp.float32
AXES = ("y", "c", "z", "x")
BF16 = jnp.bfloat16
MESH = pl.DeviceIdType.MESH
KINDS = {"C1": (1, 1, 2), "CX": (2, 1, 4), "E1": (1, 2, 2), "EX": (2, 2, 4)}
TILES = {"C1": 4, "CX": 8, "E1": 2, "EX": 4}
CLASSES = [(p, k) for p in ("own", "sib", "far") for k in KINDS if (p, k) != ("own", "C1")]
ARRIVAL = [
    ("sib", "C1"), ("own", "CX"), ("own", "E1"), ("far", "C1"), ("sib", "CX"), ("sib", "E1"),
    ("own", "EX"), ("far", "CX"), ("far", "E1"), ("sib", "EX"), ("far", "EX"),
]


def far_first(n):
    return sorted(range(1, n), key=lambda k: -min(k, n - k))


def choose(kind, table):
    low = jnp.where(kind < 0.5, table[0], table[1])
    high = jnp.where(kind < 2.5, table[2], table[3])
    return jnp.where(kind < 1.5, low, high)


def await_bytes(ref, sem):
    pltpu.make_async_copy(ref, ref, sem).wait()


class Exchange:
    def __init__(self, peers, sems, whole):
        self.peers, self.sems, self.whole = peers, sems, whole

    def start(self, src, dst):
        for k, peer in self.peers:
            pltpu.make_async_remote_copy(
                src_ref=src(k), dst_ref=dst(k), send_sem=self.sems.at[0], recv_sem=self.sems.at[1],
                device_id=peer, device_id_type=MESH,
            ).start()

    def wait(self):
        await_bytes(self.whole, self.sems.at[1])

    def finish(self):
        await_bytes(self.whole, self.sems.at[0])


def kernel(
    chi_h, eta_h, gam_h, cells_h, off_h, typ_h, out,
    chi_t, eta_t, gam_t, cells_s, cells, off, typ,
    gat, sel, rcv, hal, tgt, hbuf, hv1, hv2, acc, accx,
    rgat, rsel, rrcv, own0, az, ax, aq, msgs,
    zs, xs, qs, hs, h1s, h2s, rzs, rxs, rqs, dzs, dxs, dqs, ls,
):
    my = lax.axis_index("y")
    mc = lax.axis_index("c")
    mz = lax.axis_index("z")
    mx = lax.axis_index("x")
    mq = my * 2 + mc
    col = mz * 4 + mx
    loads = [
        pltpu.make_async_copy(src, dst, ls.at[k])
        for k, (src, dst) in enumerate((
            (off_h, off), (typ_h, typ), (chi_h, chi_t), (cells_h, cells), (cells_h, cells_s), (eta_h, eta_t), (gam_h, gam_t),
        ))
    ]
    for load in loads:
        load.start()

    zpeers = [(k, {"z": lax.rem(mz + k, NZ)}) for k in far_first(NZ)]
    xpeers = [(k, {"x": lax.rem(mx + k, NX)}) for k in far_first(NX)]
    qpeers = []
    for k in sorted(range(1, NQ), key=lambda k: -min(k, NQ - k)):
        q = lax.rem(mq + k, NQ)
        qpeers.append((k, {"y": q // 2, "c": lax.rem(q, 2)}))
    zfar = lax.rem(mz + 2 * mc - 1 + NZ, NZ)
    place = {"own": (1, mc, mz), "sib": (2 - 2 * mc, 1 - mc, mz), "far": (2 * mc, 1 - mc, zfar)}
    landing = {"own": 1, "sib": 2 * mc, "far": 2 - 2 * mc}

    def neighbours(plane, kind):
        many_x, many_y, _ = KINDS[kind]
        _, pc, pz = place[plane]
        for ex in ((0,) if many_x == 1 else (-1, 1)):
            for ey in ((0,) if many_y == 1 else (-1, 1)):
                peer = {"z": pz, "c": pc, "x": lax.rem(mx + ex + NX, NX), "y": lax.rem(my + ey + NY, NY)}
                first, n = (0, 2) if ey == 0 else ((1, 1) if ey == 1 else (0, 1))
                slot = landing[plane] * 12 + (1 - ex) * 4 + first + 1 - 2 * ey
                yield peer, first, n, slot

    barrier = pltpu.get_barrier_semaphore()
    everyone = [peer for _, peer in zpeers + xpeers + qpeers]
    for cls in CLASSES:
        everyone += [n[0] for n in neighbours(*cls)]
    for peer in everyone:
        pl.semaphore_signal(barrier, inc=1, device_id=peer, device_id_type=MESH)

    loads[0].wait()
    loads[1].wait()
    for b in range(2):
        lanes = pl.ds(b * LANES, LANES)
        for comp in range(3):
            gat[mx, mz, b, comp : comp + 1, :] = off[comp : comp + 1, lanes]
        gat[mx, mz, b, 3:4, :] = typ[b : b + 1, :].astype(F32)
    pl.semaphore_wait(barrier, len(everyone))

    zg = Exchange(zpeers, zs, gat.at[0, pl.ds(0, NZ - 1)])
    zg.start(lambda k: gat.at[mx, mz], lambda k: gat.at[mx, mz])
    for load in loads[2:]:
        load.wait()
    lane = lax.broadcasted_iota(jnp.int32, (1, LANES), 1)
    near = pl.ds(pl.multiple_of((mq // 2) * LANES, LANES), LANES)
    mine = jnp.where(lane // 64 == lax.rem(mq, 2), (cells[0:1, near] * 16 + cells[1:2, near]) * 4 + cells[2:3, near], -1)

    def key_of(q, s):
        return ((2 * mz + lax.rem(q, 2)) * 16 + 2 * (q // 2) + s) * 4 + mx

    fwd = [jnp.max(jnp.where(mine == key_of(q, s), lax.rem(lane, 64), 0)) for q in range(NQ) for s in range(2)]
    owner = []
    every = (cells[0:1, :] * 16 + cells[1:2, :]) * 4 + cells[2:3, :]
    order = lax.broadcasted_iota(jnp.int32, every.shape, 1)
    for s in range(2):
        owner.append(jnp.max(jnp.where(every == key_of(mq, s), order // 64, 0)))
    for b in range(2):
        own0[b, 0:1, :] = -choose(gat[mx, mz, b, 3:4, :], chi_t)
        own0[b, 1:2, :] = jnp.full((1, LANES), -1.0, F32)
    zg.wait()
    xg = Exchange(xpeers, xs, gat.at[pl.ds(0, NX - 1)])
    xg.start(lambda k: gat.at[mx], lambda k: gat.at[mx])
    xg.wait()

    def pick_all(source, chosen, received, wanted):
        for q in range(NQ):
            for s in range(2):
                chosen[q, s] = source[wanted(q, s)]
        received[mq] = chosen[mq]

    def gathered(i):
        at = i // 2
        return lax.rem(at, 4), at // 4, lax.rem(i, 2)

    pick_all(gat, sel, rcv, lambda q, s: gathered(fwd[q * 2 + s]))
    qg = Exchange(qpeers, qs, sel.at[pl.ds(0, NQ - 1)])
    qg.start(lambda k: sel.at[lax.rem(mq + k, NQ)], lambda k: rcv.at[mq])
    qg.wait()
    for s in range(2):
        hal[OWN + s] = rcv[owner[s], s]

    def send_halo(ref, sems):
        for plane, kind in reversed(ARRIVAL):
            for peer, first, n, slot in neighbours(plane, kind):
                pltpu.make_async_remote_copy(
                    src_ref=ref.at[pl.ds(OWN + first, n)], dst_ref=ref.at[pl.ds(slot, n)],
                    send_sem=sems.at[len(CLASSES)], recv_sem=sems.at[CLASSES.index((plane, kind))],
                    device_id=peer, device_id_type=MESH,
                ).start()

    def wait_halo(ref, sems, cls):
        await_bytes(ref.at[pl.ds(0, KINDS[cls[1]][2])], sems.at[CLASSES.index(cls)])

    def sent_halo(ref, sems):
        await_bytes(ref.at[pl.ds(0, 34)], sems.at[len(CLASSES)])

    def tiles(cls, body):
        plane, kind = place[cls[0]][0], cls[1]

        def one(k, carry):
            if kind == "C1":
                t, gz, gy = k // 2, 1, 1 + lax.rem(k, 2)
            elif kind == "CX":
                t, gz, gy = lax.rem(k // 2, 2), 2 * (k // 4), 1 + lax.rem(k, 2)
            elif kind == "E1":
                t, gz, gy = k, 1, 3 * k
            else:
                t, gz, gy = lax.rem(k, 2), 2 * (k // 2), 3 * lax.rem(k, 2)
            body(t, plane, gz, gy)
            return carry
        lax.fori_loop(0, TILES[kind], one, 0)

    send_halo(hal, hs)

    def shield_of(kind):
        gam = choose(kind, gam_t)
        return (lax.rsqrt(gam) / gam) * (0.001 ** 0.5)

    rows = []
    for t in range(2):
        rows += [(hal[OWN + t, c : c + 1, :] + (11.0 * t if c == 1 else 0.0)) * 0.1 for c in range(3)]
        rows.append(shield_of(hal[OWN + t, 3:4, :]))
    turned = jnp.concatenate(rows, axis=0).T
    for t in range(2):
        for c in range(4):
            tgt[t, c] = jnp.broadcast_to(turned[:, t * 4 + c : t * 4 + c + 1], (LANES, LANES))
    acc[...] = jnp.zeros_like(acc)

    def build(t, plane, gz, gy, diagonal=False):
        slot = plane * 12 + gz * 4 + gy
        n = plane * 9 + gz * 3 + gy - t
        step = [plane - 1, gy - 1, gz - 1]
        src = [(hal[slot, c : c + 1, :] + jnp.asarray(step[c] * 11).astype(F32)) * 0.1 for c in range(3)]
        kind = hal[slot, 3:4, :]
        shield = shield_of(kind)
        chi = choose(kind, chi_t)
        eta = choose(kind, eta_t)
        for j in range(16):
            rows = pl.ds(j * 8, 8)
            dx = src[0] - tgt[t, 0, rows, :]
            dy = src[1] - tgt[t, 1, rows, :]
            dz = src[2] - tgt[t, 2, rows, :]
            r2 = jnp.maximum(dx * dx + dy * dy + dz * dz, 1e-30)
            r = r2 * lax.rsqrt(r2)
            cube = r2 * r + shield * tgt[t, 3, rows, :]
            inv = jnp.exp2(jnp.log2(cube) * (-1.0 / 3.0))
            u = jnp.maximum(1.0 - r, 0.0)
            u = u * u
            poly = ((28.8 * r + 14.4) * r + 5.76) * r + 1.44
            h = (u * u) * poly * inv
            if diagonal:
                away = lax.broadcasted_iota(jnp.int32, (8, LANES), 1) - lax.broadcasted_iota(jnp.int32, (8, LANES), 0)
                h = jnp.where(away == j * 8 + (gy - 1 - t) * 1024, eta, h)
            hbuf[t, n, rows, :] = h
            acc[t, 0, rows, :] += h * chi
            acc[t, 1, rows, :] += h

    tiles(("own", "C1"), lambda *at: build(*at, diagonal=True))
    for cls in ARRIVAL:
        wait_halo(hal, hs, cls)
        tiles(cls, build)

    ones = jnp.ones((8, LANES), BF16)

    def across(ref, t, rhs):
        whole = ref[t, rhs]
        high = whole.astype(BF16)
        low = (whole - high.astype(F32)).astype(BF16)
        dims = (((1,), (1,)), ((), ()))
        total = [lax.dot_general(ones, part, dims, preferred_element_type=F32) for part in (high, low)]
        return (total[0] + total[1])[0:1]

    def multiply(vec, ref):
        def one(t, plane, gz, gy):
            v = vec[plane * 12 + gz * 4 + gy]
            n = plane * 9 + gz * 3 + gy - t
            for j in range(16):
                rows = pl.ds(j * 8, 8)
                h = hbuf[t, n, rows, :]
                ref[t, 0, rows, :] += h * v[0:1, :]
                ref[t, 1, rows, :] += h * v[1:2, :]
        return one

    v0 = []
    for t in range(2):
        chi = choose(hal[OWN + t, 3:4, :], chi_t)
        v0.append(jnp.concatenate([-chi, jnp.full((1, LANES), -1.0, F32)], axis=0))
        hv1[OWN + t, 0:1, :] = SHIFTS[0] * chi - across(acc, t, 0)
        hv1[OWN + t, 1:2, :] = SHIFTS[0] - across(acc, t, 1)
    send_halo(hv1, h1s)
    accx[...] = jnp.zeros_like(accx)
    for e in (zg, xg, qg):
        e.finish()
    sent_halo(hal, hs)
    tiles(("own", "C1"), multiply(hv1, accx))
    for cls in ARRIVAL:
        wait_halo(hv1, h1s, cls)
        tiles(cls, multiply(hv1, accx))
    for t in range(2):
        for rhs in range(2):
            hv2[OWN + t, rhs : rhs + 1, :] = across(accx, t, rhs) - SHIFTS[1] * hv1[OWN + t, rhs : rhs + 1, :]
    send_halo(hv2, h2s)
    for t in range(2):
        rgat[mx, mz, t, 0:2, :] = hv1[OWN + t]
        rgat[mx, mz, t, 2:4, :] = hv2[OWN + t]
    rz = Exchange(zpeers, rzs, rgat.at[0, pl.ds(0, NZ - 1)])
    rz.start(lambda k: rgat.at[mx, mz], lambda k: rgat.at[mx, mz])
    acc[...] = jnp.zeros_like(acc)
    tiles(("own", "C1"), multiply(hv2, acc))

    lane2 = lax.broadcasted_iota(jnp.int32, (2, LANES), 1)
    v = [v0, [hv1[OWN + t] for t in range(2)], [hv2[OWN + t] for t in range(2)]]
    terms = [v[a][0] * v[b][0] + v[a][1] * v[b][1] for a, b in ((0, 0), (0, 1), (0, 2), (1, 1), (1, 2), (2, 2))]
    terms += [None] + [v[a][0] + v[a][1] for a in range(3)]
    msg = jnp.zeros((2, LANES), F32)
    for k, term in enumerate(terms):
        if term is not None:
            msg = jnp.where(lane2 == k, jnp.sum(term, axis=1, keepdims=True), msg)
    sent_halo(hv1, h1s)
    for cls in ARRIVAL:
        wait_halo(hv2, h2s, cls)
        tiles(cls, multiply(hv2, acc))
    image = [jnp.concatenate([across(acc, t, 0), across(acc, t, 1)], axis=0) for t in range(2)]
    term = v[2][0] * image[0] + v[2][1] * image[1]
    msg = jnp.where(lane2 == 6, jnp.sum(term, axis=1, keepdims=True), msg)
    msgs[0] = msg
    az[mz] = msg
    dz_ = Exchange(zpeers, dzs, az.at[pl.ds(0, NZ - 1)])
    dz_.start(lambda k: msgs.at[0], lambda k: az.at[mz])
    rz.wait()
    rx = Exchange(xpeers, rxs, rgat.at[pl.ds(0, NX - 1)])
    rx.start(lambda k: rgat.at[mx], lambda k: rgat.at[mx])
    sent_halo(hv2, h2s)
    rz.finish()

    def lies(b):
        cx, cy, cz = cells_s[0, b], cells_s[1, b], cells_s[2, b]
        return (cz, cx // 2, lax.rem(cy, 2)), (cy // 2) * 2 + lax.rem(cx, 2)

    back_at = [lies(q * 64 + col * 2 + s)[0] for q in range(NQ) for s in range(2)]
    holder = [lies(mq * 64 + col * 2 + s)[1] for s in range(2)]
    dz_.wait()
    msg = az[0]
    for k in range(1, NZ):
        msg = msg + az[k]
    msgs[1] = msg
    ax[mx] = msg
    dx_ = Exchange(xpeers, dxs, ax.at[pl.ds(0, NX - 1)])
    dx_.start(lambda k: msgs.at[1], lambda k: ax.at[mx])
    rx.wait()
    pick_all(rgat, rsel, rrcv, lambda q, s: back_at[q * 2 + s])
    rq = Exchange(qpeers, rqs, rsel.at[pl.ds(0, NQ - 1)])
    rq.start(lambda k: rsel.at[lax.rem(mq + k, NQ)], lambda k: rrcv.at[mq])
    dx_.wait()
    msg = ax[0]
    for k in range(1, NX):
        msg = msg + ax[k]
    msgs[2] = msg
    aq[mq] = msg
    dq_ = Exchange(qpeers, dqs, aq.at[pl.ds(0, NQ - 1)])
    dq_.start(lambda k: msgs.at[2], lambda k: aq.at[mq])
    for e in (rx, dz_, dx_):
        e.finish()
    rq.wait()
    rq.finish()
    back = [rrcv[holder[s], s] for s in range(2)]
    dq_.wait()
    msg = aq[0]
    for k in range(1, NQ):
        msg = msg + aq[k]

    m = [jnp.broadcast_to(msg[:, k : k + 1], (2, LANES)) for k in range(MOMENTS)]
    gram = {(0, 0): m[0], (0, 1): m[1], (0, 2): m[2], (1, 1): m[3], (1, 2): m[4], (2, 2): m[5]}
    sums = m[7:]

    def dot(i, j):
        return gram[min(i, j), max(i, j)]

    def image_dot(i, j):
        i, j = min(i, j), max(i, j)
        return m[6] if i == 2 else dot(i + 1, j) + SHIFTS[i] * dot(i, j)

    def quadratic(a, form):
        total = None
        for i, ai in enumerate(a):
            for j in range(i, len(a)):
                term = ai * a[j] * form(i, j)
                term = term if i == j else term + term
                total = term if total is None else total + term
        return total

    def image(a):
        res = [None] * (len(a) + 1)
        for i, ai in enumerate(a):
            res[i + 1] = ai
            res[i] = SHIFTS[i] * ai if res[i] is None else res[i] + SHIFTS[i] * ai
        return res

    def plus(a, scale, b):
        res = []
        for i in range(max(len(a), len(b))):
            ai = a[i] if i < len(a) else None
            bi = b[i] if i < len(b) else None
            if bi is None:
                res.append(ai)
            elif ai is None:
                res.append(scale * bi)
            else:
                res.append(ai + scale * bi)
        return res

    one = jnp.ones((2, LANES), F32)
    x, r, p = [], [one], [one]
    rr = m[0]
    for step in range(3):
        alpha = rr / quadratic(p, image_dot)
        x = plus(x, alpha, p)
        if step < 2:
            r = plus(r, -alpha, image(p))
            new = quadratic(r, dot)
            p = plus(r, new / rr, p)
            rr = new
    total = x[0] * sums[0] + x[1] * sums[1] + x[2] * sums[2]
    ratio = total[0:1] / total[1:2]
    for s in range(2):
        b = back[s]
        part = x[0] * own0[s] + x[1] * b[0:2] + x[2] * b[2:4]
        out[s : s + 1, :] = part[0:1] - ratio * part[1:2]
    dq_.finish()


def per_device(offsets, cells, types, mask, chi_table, eta_table, gamma_table):
    def vmem(*shape):
        return pltpu.VMEM(shape, F32)

    def sems(n=2):
        return pltpu.SemaphoreType.DMA((n,))

    table = pltpu.SMEM((4,), F32)
    charges = pl.pallas_call(
        kernel,
        out_shape=jax.ShapeDtypeStruct((2, LANES), F32),
        in_specs=[pl.BlockSpec(memory_space=pl.ANY)] * 6,
        out_specs=pl.BlockSpec(memory_space=pltpu.VMEM),
        scratch_shapes=[
            table, table, table, pltpu.SMEM(cells.shape, jnp.int32), pltpu.VMEM(cells.shape, jnp.int32),
            vmem(3, 2 * LANES), pltpu.VMEM((2, LANES), jnp.int32),
            vmem(NX, NZ, 2, 4, LANES), vmem(NQ, 2, 4, LANES), vmem(NQ, 2, 4, LANES),
            vmem(SLOTS, 4, LANES), vmem(2, 4, LANES, LANES), vmem(2, PAIRS, LANES, LANES),
            vmem(SLOTS, 2, LANES), vmem(SLOTS, 2, LANES), vmem(2, 2, LANES, LANES), vmem(2, 2, LANES, LANES),
            vmem(NX, NZ, 2, 4, LANES), vmem(NQ, 2, 4, LANES), vmem(NQ, 2, 4, LANES),
            vmem(2, 2, LANES), vmem(NZ, 2, LANES), vmem(NX, 2, LANES), vmem(NQ, 2, LANES), vmem(3, 2, LANES),
            *[sems()] * 3, *[sems(len(CLASSES) + 1)] * 3, *[sems()] * 6, sems(7),
        ],
        compiler_params=pltpu.CompilerParams(collective_id=0, has_side_effects=True),
    )(chi_table, eta_table, gamma_table, cells, offsets, types.reshape(2, LANES))
    return charges.reshape(2 * LANES)


def solution(mesh):
    torus = Mesh(mesh.devices.reshape(8, 2, 8, 4), AXES)
    placed = (P(None, AXES), P(), P(AXES), P(None, ("z", "x"), ("y", "c"), None), P(), P(), P())
    return jax.shard_map(
        per_device, mesh=torus, in_specs=placed, out_specs=P(AXES), check_vma=False
    )
```

time: 74.4 us -> 62 us (0.83)
  Pallas kernels: 70 us -> 60.6 us
  local copies, waits for them, and re-layouts: 3.25 us -> 1.22 us
  other arithmetic: 0.83 us -> 0 us
    pallas_call x1, Pallas kernels: 70 us -> 60.6 us  [per_device(): pl.pallas_call(kernel, out_shape=jax.ShapeDtypeStruct((2, LANES), F32), i...]
    unnamed x6 -> x3, local copies, waits for them, and re-layouts: 1.88 us -> 1.22 us
where the time goes in v2:
time: 62 us; the launch traced here: 61.9 us
  Pallas kernels  60.6 us (98%)
  local copies, waits for them, and re-layouts  1.22 us (2%)
    pallas_call x1, Pallas kernels, per_device(): pl.pallas_call(kernel, out_shape=jax.ShapeDtypeStruct((2, LANES), F32), i...  60.6 us

profile of v2, /device:TPU:1, one launch (start us, length us, event | category | flops | bytes accessed | tf_op | source)
XLA Modules:
  0.0 61.9 jit_solution(11769515294140825808)
XLA Ops:
  0.0 60.6 %shard_map.64 = f32[2,128]{1,0:T(2,128)} custom-call(f32[4]{0:T(128)} %chi_h.1, f32[4]{0:T(128)} %eta_h.1, f32[4]{0:T(128)} %gam_h.1, s32[3,1024]{1,0:T(4,128)} %cells_h.1, f32[3,256]{1,0:T(4,128)} %off_h.1, s32[2,128]{1,0:T(2,128)} %bitcast.3), custom_call_target="tpu_custom_call" | custom-call | tf_op jit(solution)/shard_map/pallas_call | solution.py:419
  60.6 0.0 copy-start
  60.7 0.7 %copy-done = f32[2,128]{1,0:T(2,128)S(1)} copy-done((f32[2,128]{1,0:T(2,128)S(1)}, f32[2,128]{1,0:T(2,128)}, u32[]{:S(2)}) %copy-start) | copy-done | bytes 1048
  61.3 0.6 copy.8
Async XLA Ops:
  60.6 0.7 %copy-start = (f32[2,128]{1,0:T(2,128)S(1)}, f32[2,128]{1,0:T(2,128)}, u32[]{:S(2)}) copy-start(f32[2,128]{1,0:T(2,128)} %shard_map.64) | copy-start | bytes 3076
